TPU v7x, 32 devices: a whole 2x2x4 slice. The times are simulated.
32 devices in a mesh: row: 4 (over x, core), col: 8 (over z, y).
Axes of the slice: x: 2, y: 2, z: 4, core: 2. Of those that a mesh axis runs over, the one named last changes fastest.
Arguments:
- jump: float32 [3, 256, 1024], P(None, 'row', 'col'), may hold values from -6 to 6
- external: float32 [3, 256, 1024], P(None, 'row', 'col'), may hold values from -12 to 12
- cohesive: float32 [256, 1024], P('row', 'col'), may hold values from 0.5 to 4
- bond_mask: int32 [2, 256, 1024], P(None, 'row', 'col'), may hold values 0 or 1
- load_factor: float32 [1], replicated, may hold values from 0.5 to 1.5
- arc_radius: float32 [1], replicated, may hold values from 0.5 to 1.5
- stiffness: bfloat16 [1536, 1536], replicated, may hold values from -1 to 2
- coupling: float32 [3, 1536], replicated, may hold values from -6 to 6
- old_state: float32 [5120, 1536], P(('row', 'col')), may hold values from -3 to 3
- old_history: float32 [5120, 1536], P(('row', 'col')), may hold values from 0 to 1.5
- newton_steps: int32 [5120], P(('row', 'col')), may hold values from 0 to 9, as said below
- point_ids: int32 [5120], P(('row', 'col')), may hold values from 0 to 8191, as said below
Outputs:
- new_jump: float32 [3, 256, 1024], P(None, 'row', 'col')
- new_load: float32 [1], replicated
- new_state: float32 [2560, 1536], P(('row', 'col'))
- new_history: float32 [2560, 1536], P(('row', 'col'))
Inputs may be any that keep to these rules, and one draw needn't show every extreme that they name: `newton_steps`: within one block the live slots number between 20 and 160, and some block has all 160 live; in all at most 2240 slots are live; a live slot's count is at least 2. `point_ids`: the slots of one block name distinct points of that block.
All inputs are finite; a program needn't handle non-finite values. No bound on the sum of `bond_mask` on one device may be relied on, other than what follows from the above.
Results may differ from a plain program's by a relative error of at most 0.0028.
Values sent between devices are 32-bit elements; how exact they have to be, the bound alone decides.
A program may use at most 64 MiB of HBM per device.

v0:
```python
import functools

import jax
import jax.numpy as jnp
from jax import lax
from jax.experimental import pallas as pl
from jax.experimental.pallas import tpu as pltpu
from jax.sharding import PartitionSpec as P

MAX_STEPS = 9
SWEEPS = 3
TILE = 256
LANES = 128
MESH = pl.DeviceIdType.MESH
F32 = jnp.float32
BF16 = jnp.bfloat16


def iota(shape, dim):
    return lax.broadcasted_iota(jnp.int32, shape, dim)


def picked(onehot, values):
    high = values.astype(BF16)
    rest = values - high.astype(F32)
    middle = rest.astype(BF16)
    low = (rest - middle.astype(F32)).astype(BF16)
    dot = functools.partial(jnp.dot, preferred_element_type=F32)
    return dot(onehot, high) + dot(onehot, middle) + dot(onehot, low)


def body(
    nrow,
    ncol,
    pair,
    jump_ref,
    external_ref,
    cohesive_ref,
    bond_ref,
    load_ref,
    radius_ref,
    coupling_ref,
    steps_ref,
    points_ref,
    stiffness_hbm,
    state_hbm,
    history_hbm,
    new_jump_ref,
    new_load_ref,
    new_state_ref,
    new_history_ref,
    stiff,
    state,
    history,
    damage,
    load,
    rounded,
    diagonal,
    count_out,
    count_in,
    sum_out,
    sum_in,
    x_out,
    x_in,
    y_out,
    y_in,
    out_history,
    in_history,
    out_state,
    in_state,
    local_sems,
    halo_send,
    halo_recv,
    all_send,
    all_recv,
):
    devices = nrow * ncol
    row, col = lax.axis_index("row"), lax.axis_index("col")
    here = row * ncol + col
    slots, cells = state.shape
    X, Y = cohesive_ref.shape
    new_cap = new_state_ref.shape[0]
    padded = out_history.shape[1]
    width = devices * padded
    bits = devices.bit_length() - 1

    fetch = [
        pltpu.make_async_copy(history_hbm, history, local_sems.at[0]),
        pltpu.make_async_copy(stiffness_hbm, stiff, local_sems.at[1]),
        pltpu.make_async_copy(state_hbm, state, local_sems.at[2]),
    ]
    for copy in fetch:
        copy.start()

    def peer(k):
        p = lax.rem(here + k, devices)
        return {"row": lax.div(p, ncol), "col": lax.rem(p, ncol)}, p

    x_in[...] = jnp.zeros_like(x_in)
    y_in[...] = jnp.zeros_like(y_in)
    if pair < padded:
        blank = jnp.zeros((devices, padded - pair, cells), F32)
        in_history[:, pair:, :] = blank
        in_state[:, pair:, :] = blank

    steps_row = steps_ref[...]
    live_row = (steps_row > 0).astype(F32)
    count_out[...] = jnp.broadcast_to(jnp.sum(live_row, axis=1, keepdims=True), count_out.shape)

    lane = iota((X, Y), 1)
    line = iota((X, Y), 0)

    def stage(phase, fields):
        right = jnp.zeros((X, Y), F32)
        left = jnp.zeros((X, Y), F32)
        for c, (x_field, y_field) in enumerate(fields):
            x_out[phase, 0, c : c + 1, :] = x_field[X - 1 : X, :]
            x_out[phase, 1, c : c + 1, :] = x_field[0:1, :]
            right = jnp.where(lane == c, pltpu.roll(y_field, (c + 1) % Y, 1), right)
            left = jnp.where(lane == c, pltpu.roll(y_field, c, 1), left)
        y_out[phase, 0] = right
        y_out[phase, 1] = left

    def halo_copies(phase):
        plan = (
            (x_out, x_in, 0, row < nrow - 1, row > 0, {"row": row + 1, "col": col}),
            (x_out, x_in, 1, row > 0, row < nrow - 1, {"row": row - 1, "col": col}),
            (y_out, y_in, 0, col < ncol - 1, col > 0, {"row": row, "col": col + 1}),
            (y_out, y_in, 1, col > 0, col < ncol - 1, {"row": row, "col": col - 1}),
        )
        copies = []
        for index, (source, target, way, sends, gets, device) in enumerate(plan):
            copy = pltpu.make_async_remote_copy(
                src_ref=source.at[phase, way],
                dst_ref=target.at[phase, way],
                send_sem=halo_send.at[phase, index],
                recv_sem=halo_recv.at[phase, index],
                device_id=device,
                device_id_type=MESH,
            )
            copies.append((copy, sends, gets))
        return copies

    def halo_start(phase):
        for copy, sends, _ in halo_copies(phase):
            pl.when(sends)(copy.start)

    def halo_wait(phase):
        for copy, sends, gets in halo_copies(phase):
            pl.when(gets)(copy.wait_recv)

    def halo_wait_sends(phase):
        for copy, sends, gets in halo_copies(phase):
            pl.when(sends)(copy.wait_send)

    def spread(source_of, target, kind, first, last):
        def one(k, carry):
            device, p = peer(k)
            pltpu.make_async_remote_copy(
                src_ref=source_of(p),
                dst_ref=target,
                send_sem=all_send.at[kind],
                recv_sem=all_recv.at[kind],
                device_id=device,
                device_id_type=MESH,
            ).start()
            return carry

        lax.fori_loop(first, last, one, 0)

    def spread_wait(buffer, sem):
        pltpu.make_async_copy(buffer, buffer, sem).wait()

    bond_x = 0.25 + 0.75 * bond_ref[0].astype(F32)
    bond_y = 0.25 + 0.75 * bond_ref[1].astype(F32)
    jump = [jump_ref[c] for c in range(3)]
    stage(0, [(jump[c], jump[c]) for c in range(3)] + [(bond_x, bond_y)])

    barrier = pltpu.get_barrier_semaphore()

    def greet(k, carry):
        device, _ = peer(k)
        pl.semaphore_signal(barrier, inc=1, device_id=device, device_id_type=MESH)
        return carry

    lax.fori_loop(1, devices, greet, 0)
    pl.semaphore_wait(barrier, devices - 1)

    count_in[pl.ds(here, 1)] = count_out[...][None]
    spread(lambda p: count_out, count_in.at[here], 0, 1, devices)
    halo_start(0)

    slot_line = iota((slots, slots), 0)
    slot_lane = iota((slots, slots), 1)

    def to_column(values):
        return jnp.sum(jnp.where(slot_line == slot_lane, values, 0.0), axis=1, keepdims=True)

    points_row = points_ref[...]
    px_row = lax.shift_right_logical(points_row, (Y.bit_length() - 1))
    py_row = points_row & (Y - 1)
    px_col = to_column(px_row.astype(F32)).astype(jnp.int32)
    py_col = to_column(py_row.astype(F32)).astype(jnp.int32)
    steps_col = to_column(steps_row.astype(F32)).astype(jnp.int32)
    live_col = (steps_col > 0).astype(F32)
    at_x = (iota((slots, X), 1) == px_col).astype(F32).astype(BF16)
    at_y = (iota((slots, Y), 1) == py_col).astype(F32)
    at_x_turned = (iota((X, slots), 0) == px_row).astype(F32).astype(BF16)
    drive = []
    for c in range(3):
        lines = picked(at_x, jump[c])
        drive.append(jnp.sum(lines * at_y, axis=1, keepdims=True))
    for start in range(0, cells, TILE):
        part = slice(start, start + TILE)
        total = drive[0] * coupling_ref[0:1, part]
        total = total + drive[1] * coupling_ref[1:2, part]
        load[:, part] = total + drive[2] * coupling_ref[2:3, part]
    rank_row = jnp.sum(jnp.where(slot_line < slot_lane, live_col, 0.0), axis=0, keepdims=True)

    fetch[0].wait()
    for start in range(0, cells, TILE):
        part = slice(start, start + TILE)
        damage[:, part] = jnp.exp(-history[:, part])

    spread_wait(count_in.at[pl.ds(0, devices - 1)], all_recv.at[0])
    counts = jnp.max(count_in[...], axis=1)
    device_line = iota((devices, LANES), 0)
    device_lane = iota((devices, LANES), 1)
    starts = jnp.sum(jnp.where(device_line < device_lane, counts, 0.0), axis=0, keepdims=True)
    ends = jnp.sum(jnp.where(device_line <= device_lane, counts, 0.0), axis=0, keepdims=True)
    my_start = jnp.sum(jnp.where(device_line < here, counts, 0.0), axis=0, keepdims=True)[:, :1]
    my_start = my_start.astype(jnp.int32)

    def place(rank, first):
        pairs = lax.shift_right_logical(rank, 1) - lax.shift_right_logical(first, 1)
        return 2 * lax.shift_right_logical(pairs, bits) + (rank & 1)

    ranks = rank_row.astype(jnp.int32) + my_start
    home = lax.shift_right_logical(ranks, 1) & (devices - 1)
    leaves = jnp.where(steps_row > 0, home * padded + place(ranks, my_start), -1)
    leaving = (iota((width, slots), 0) == leaves).astype(F32).astype(BF16)

    wanted_slot = iota((new_cap, LANES), 0)
    wanted = 2 * (here + devices * lax.shift_right_logical(wanted_slot, 1)) + (wanted_slot & 1)
    wanted_lane = iota((new_cap, LANES), 1)
    wanted_float = wanted.astype(F32)
    hit = (starts <= wanted_float) & (wanted_float < ends) & (wanted_lane < devices)
    valid = jnp.sum(jnp.where(hit, 1.0, 0.0), axis=1, keepdims=True)
    from_start = jnp.sum(jnp.where(hit, starts, 0.0), axis=1, keepdims=True).astype(jnp.int32)
    source = jnp.sum(jnp.where(hit, wanted_lane.astype(F32), 0.0), axis=1, keepdims=True)
    arrives = source.astype(jnp.int32) * padded + place(wanted[:, :1], from_start)
    arrives = jnp.where(valid > 0.0, arrives, -1)
    coming = (iota((new_cap, width), 1) == arrives).astype(F32).astype(BF16)

    def gather_out(values, out, inside):
        for start in range(0, cells, TILE):
            part = slice(start, start + TILE)
            rows = picked(leaving, values[:, part])
            out[:, :, part] = rows.reshape(devices, padded, TILE)
        inside[pl.ds(here, 1)] = out[pl.ds(here, 1)]

    gather_out(history, out_history, in_history)
    row_part = pl.ds(0, pair)
    spread(
        lambda p: out_history.at[p, row_part], in_history.at[here, row_part], 1, 1, devices
    )

    fetch[1].wait()
    fetch[2].wait()
    tile_eye = iota((TILE, TILE), 0) == iota((TILE, TILE), 1)
    for start in range(0, cells, TILE):
        part = slice(start, start + TILE)
        block = stiff[part, part].astype(F32)
        diagonal[:, part] = jnp.sum(jnp.where(tile_eye, block, 0.0), axis=0, keepdims=True)
        rounded[0, :, part] = state[:, part].astype(BF16)

    def advance(count, carry):
        now = lax.rem(count, 2)
        moves = count < steps_col
        for start in range(0, cells, TILE):
            part = slice(start, start + TILE)
            force = jnp.dot(rounded[now], stiff[:, part], preferred_element_type=F32)
            current = state[:, part]
            bent = jnp.tanh(current)
            worn = damage[:, part]
            misfit = force + worn * bent - load[:, part]
            slope = diagonal[:, part] + worn * (1.0 - bent * bent)
            current = jnp.where(moves, current - misfit / slope, current)
            state[:, part] = current
            rounded[1 - now, :, part] = current.astype(BF16)
        return carry

    lax.fori_loop(0, MAX_STEPS, advance, 0)

    others = devices - 1
    bounds = [1] + [1 + others * s // 20 for s in (4, 10, 15)] + [devices]

    def send_state(step):
        spread(
            lambda p: out_state.at[p, row_part],
            in_state.at[here, row_part],
            2,
            bounds[step],
            bounds[step + 1],
        )

    gather_out(state, out_state, in_state)
    send_state(0)

    first_sum = jnp.zeros((slots, 16), F32)
    second_sum = jnp.zeros((slots, 16), F32)
    turned = (((1,), (1,)), ((), ()))

    def split(values):
        high = values.astype(BF16)
        return high, (values - high.astype(F32)).astype(BF16)

    def summed(values, factors):
        high, low = split(values)
        both = factors.astype(BF16).astype(F32)
        both = jnp.concatenate([both, factors - both], axis=0).astype(BF16)
        dot = functools.partial(
            lax.dot_general, dimension_numbers=turned, preferred_element_type=F32
        )
        return dot(high, both) + dot(low, both)

    for start in range(0, cells, TILE):
        part = slice(start, start + TILE)
        bent = jnp.tanh(state[:, part])
        worn = damage[:, part]
        a0, a1, a2 = [coupling_ref[a : a + 1, part] for a in range(3)]
        none = jnp.zeros((2, TILE), F32)
        firsts = jnp.concatenate([a0, a1, a2, none, none, none[:1]], axis=0)
        seconds = jnp.concatenate(
            [a0 * a0, a1 * a1, a2 * a2, a0 * a1, a0 * a2, a1 * a2, none], axis=0
        )
        first_sum = first_sum + summed(worn * bent, firsts)
        second_sum = second_sum + summed(worn * (1.0 - bent * bent), seconds)
    first_sum = (first_sum[:, :8] + first_sum[:, 8:]) * (live_col / cells)
    second_sum = (second_sum[:, :8] + second_sum[:, 8:]) * (live_col / cells)

    def put(values):
        return picked(at_x_turned, at_y * values)

    soft = put(live_col)
    rve_traction = [put(first_sum[:, c : c + 1]) for c in range(3)]
    tangent = [put(second_sum[:, c : c + 1]) for c in range(6)]

    halo_wait(0)

    def before_x(phase, field, c):
        return jnp.where(line == 0, x_in[phase, 0, c : c + 1, :], pltpu.roll(field, 1, 0))

    def after_x(phase, field, c):
        return jnp.where(line == X - 1, x_in[phase, 1, c : c + 1, :], pltpu.roll(field, X - 1, 0))

    def before_y(phase, field, c):
        edge = pltpu.roll(y_in[phase, 0], (Y - c) % Y, 1)
        return jnp.where(lane == 0, edge, pltpu.roll(field, 1, 1))

    def after_y(phase, field, c):
        edge = pltpu.roll(y_in[phase, 1], Y - 1 - c, 1)
        return jnp.where(lane == Y - 1, edge, pltpu.roll(field, Y - 1, 1))

    low_x = before_x(0, bond_x, 3)
    low_y = before_y(0, bond_y, 3)

    def neighbours(phase, field, c):
        return (
            bond_x * after_x(phase, field, c)
            + low_x * before_x(phase, field, c)
            + bond_y * after_y(phase, field, c)
            + low_y * before_y(phase, field, c)
        )

    scale = bond_x + low_x + bond_y + low_y + (1.0 - soft) * cohesive_ref[...]
    terms = []
    for c in range(3):
        residual = (
            scale * jump[c]
            - neighbours(0, jump[c], c)
            + rve_traction[c]
            - load_ref[0] * external_ref[c]
        )
        terms.append(-residual)
    for c in range(3):
        terms.append(external_ref[c])
    d00, d11, d22 = [scale + tangent[c] for c in range(3)]
    d01, d02, d12 = tangent[3:]
    c00 = d11 * d22 - d12 * d12
    c11 = d00 * d22 - d02 * d02
    c22 = d00 * d11 - d01 * d01
    c01 = d02 * d12 - d01 * d22
    c02 = d01 * d12 - d02 * d11
    c12 = d01 * d02 - d00 * d12
    inverse = 1.0 / (d00 * c00 + d01 * c01 + d02 * c02)
    c00, c11, c22, c01, c02, c12 = [c * inverse for c in (c00, c11, c22, c01, c02, c12)]

    def solve_both(w):
        result = []
        for h in (0, 3):
            result.append(c00 * w[h] + c01 * w[h + 1] + c02 * w[h + 2])
            result.append(c01 * w[h] + c11 * w[h + 1] + c12 * w[h + 2])
            result.append(c02 * w[h] + c12 * w[h + 1] + c22 * w[h + 2])
        return result

    iterate = solve_both(terms)
    peers = pl.ds(0, devices - 1)
    for sweep in range(SWEEPS):
        phase = sweep + 1
        stage(phase, [(v, v) for v in iterate])
        halo_start(phase)
        send_state(sweep + 1)
        if sweep == 0:
            spread_wait(in_history.at[peers, row_part], all_recv.at[1])
            for start in range(0, cells, TILE):
                part = slice(start, start + TILE)
                kept = picked(coming, in_history[:, :, part].reshape(width, TILE))
                new_history_ref[:, part] = kept
        halo_wait(phase)
        iterate = solve_both([terms[c] + neighbours(phase, iterate[c], c) for c in range(6)])
    correction, direction = iterate[:3], iterate[3:]

    def total_of(fields):
        return jnp.sum(fields[0] + fields[1] + fields[2], axis=0, keepdims=True)

    cross_row = total_of([correction[c] * direction[c] for c in range(3)])
    square_row = total_of([direction[c] * direction[c] for c in range(3)])
    sum_out[...] = jnp.where(iota((8, Y), 0) == 0, cross_row, square_row)
    sum_in[pl.ds(here, 1)] = sum_out[...][None]
    spread(lambda p: sum_out, sum_in.at[here], 3, 1, devices)
    spread_wait(sum_in.at[pl.ds(0, devices - 1)], all_recv.at[3])
    sums = jnp.sum(sum_in[...], axis=0)
    cross = jnp.sum(sums[0:1, :], axis=1, keepdims=True)
    square = jnp.sum(sums[1:2, :], axis=1, keepdims=True)
    entries = 3.0 * X * Y * devices
    shifted = square + 0.25 * entries
    root = jnp.sqrt(shifted) * (entries**0.5)
    increment = (radius_ref[0] * root - cross) / shifted
    for c in range(3):
        new_jump_ref[c] = jump[c] + correction[c] + increment * direction[c]
    new_load_ref[...] = load_ref[0] + increment

    spread_wait(in_state.at[peers, row_part], all_recv.at[2])
    for start in range(0, cells, TILE):
        part = slice(start, start + TILE)
        moved = picked(coming, in_state[:, :, part].reshape(width, TILE))
        new_state_ref[:, part] = moved
        new_history_ref[:, part] = jnp.maximum(new_history_ref[:, part], jnp.abs(moved))

    for phase in range(SWEEPS + 1):
        halo_wait_sends(phase)
    spread_wait(count_in.at[peers], all_send.at[0])
    spread_wait(out_history.at[peers, row_part], all_send.at[1])
    spread_wait(out_state.at[peers, row_part], all_send.at[2])
    spread_wait(sum_in.at[peers], all_send.at[3])


def on_device(
    jump,
    external,
    cohesive,
    bond_mask,
    load_factor,
    arc_radius,
    stiffness,
    coupling,
    old_state,
    old_history,
    newton_steps,
    point_ids,
):
    nrow, ncol = lax.axis_size("row"), lax.axis_size("col")
    devices = nrow * ncol
    slots, cells = old_state.shape
    X, Y = cohesive.shape
    new_cap = slots // 2
    pair = 2 * ((slots + 2 * devices + 1) // (2 * devices))
    padded = 8 * ((pair + 7) // 8)
    phases = SWEEPS + 1
    vmem = pl.BlockSpec(memory_space=pltpu.VMEM)
    smem = pl.BlockSpec(memory_space=pltpu.SMEM)
    hbm = pl.BlockSpec(memory_space=pl.ANY)
    new_jump, new_load, new_state, new_history = pl.pallas_call(
        functools.partial(body, nrow, ncol, pair),
        out_shape=(
            jax.ShapeDtypeStruct(jump.shape, F32),
            jax.ShapeDtypeStruct((1, 1), F32),
            jax.ShapeDtypeStruct((new_cap, cells), F32),
            jax.ShapeDtypeStruct((new_cap, cells), F32),
        ),
        in_specs=[vmem] * 4 + [smem] * 2 + [vmem] * 3 + [hbm] * 3,
        out_specs=(vmem,) * 4,
        scratch_shapes=[
            pltpu.VMEM((cells, cells), BF16),
            pltpu.VMEM((slots, cells), F32),
            pltpu.VMEM((slots, cells), F32),
            pltpu.VMEM((slots, cells), F32),
            pltpu.VMEM((slots, cells), F32),
            pltpu.VMEM((2, slots, cells), BF16),
            pltpu.VMEM((1, cells), F32),
            pltpu.VMEM((8, LANES), F32),
            pltpu.VMEM((devices, 8, LANES), F32),
            pltpu.VMEM((8, Y), F32),
            pltpu.VMEM((devices, 8, Y), F32),
            pltpu.VMEM((phases, 2, 8, Y), F32),
            pltpu.VMEM((phases, 2, 8, Y), F32),
            pltpu.VMEM((phases, 2, X, Y), F32),
            pltpu.VMEM((phases, 2, X, Y), F32),
            pltpu.VMEM((devices, padded, cells), F32),
            pltpu.VMEM((devices, padded, cells), F32),
            pltpu.VMEM((devices, padded, cells), F32),
            pltpu.VMEM((devices, padded, cells), F32),
            pltpu.SemaphoreType.DMA((3,)),
            pltpu.SemaphoreType.DMA((phases, 4)),
            pltpu.SemaphoreType.DMA((phases, 4)),
            pltpu.SemaphoreType.DMA((4,)),
            pltpu.SemaphoreType.DMA((4,)),
        ],
        compiler_params=pltpu.CompilerParams(
            collective_id=0, has_side_effects=True, vmem_limit_bytes=60 * 1024 * 1024
        ),
    )(
        jump,
        external,
        cohesive,
        bond_mask,
        load_factor,
        arc_radius,
        coupling,
        newton_steps.reshape(1, slots),
        point_ids.reshape(1, slots),
        stiffness,
        old_state,
        old_history,
    )
    return new_jump, new_load.reshape(1), new_state, new_history


def solution(mesh):
    in_specs = (
        P(None, "row", "col"),
        P(None, "row", "col"),
        P("row", "col"),
        P(None, "row", "col"),
        P(),
        P(),
        P(),
        P(),
        P(("row", "col"), None),
        P(("row", "col"), None),
        P(("row", "col")),
        P(("row", "col")),
    )
    out_specs = (P(None, "row", "col"), P(), P(("row", "col"), None), P(("row", "col"), None))
    return jax.shard_map(
        on_device, mesh=mesh, in_specs=in_specs, out_specs=out_specs, check_vma=False
    )
```

profile of v0, /device:TPU:0, one launch (start us, length us, event | category | flops | bytes accessed | tf_op | source)
XLA Modules:
  0.0 83.4 jit_solution(17747595179517195398)
XLA Ops:
  1.9 74.5 %shard_map.147 = (f32[3,64,128]{2,1,0:T(8,128)}, f32[1,1]{1,0:T(1,128)}, f32[80,1536]{1,0:T(8,128)}, f32[80,1536]{1,0:T(8,128)}) custom-call(f32[3,64,128]{2,1,0:T(8,128)} %jump_ref.1, f32[3,64,128]{2,1,0:T(8,128)} %external_ref.1, f32[64,128]{1,0:T(8,128)} %cohesive_ref.1, s32[2,64,128]{2,1,0:T(8,128)} %bond_ref.1, f32[1]{0:T(128)S(6)} %copy.20.load_ref, ...), custom_call_target="tpu_custom_call" | custom-call | tf_op jit(solution)/shard_map/pallas_call | solution.py:484
  76.4 1.5 %copy.22 = f32[3,64,128]{2,1,0:T(8,128)} copy(f32[3,64,128]{2,1,0:T(8,128)} %get-tuple-element.16) | data formatting | bytes 196608
  78.6 1.8 %copy.24 = f32[80,1536]{1,0:T(8,128)} copy(f32[80,1536]{1,0:T(8,128)} %get-tuple-element.18) | data formatting | bytes 983040
  80.5 1.8 %copy.25 = f32[80,1536]{1,0:T(8,128)} copy(f32[80,1536]{1,0:T(8,128)} %get-tuple-element.19) | data formatting | bytes 983040
where the time goes:
time: 83.7 us; the launch traced here: 83.4 us
  Pallas kernels  74.5 us (89%)
  local copies, waits for them, and re-layouts  5.23 us (6%)
  between operations  3.7 us (4%)
    pallas_call x1, Pallas kernels, on_device(): pl.pallas_call(functools.partial(body, nrow, ncol, pair), out_shape=(jax....  74.5 us
    unnamed x3, local copies, waits for them, and re-layouts  5.23 us

commit v1 on v0

--- a/solution.py
+++ b/solution.py
@@ -10,6 +10,8 @@
 MAX_STEPS = 9
 SWEEPS = 3
 TILE = 256
+EARLY = 1
+CHUNKS = (5, 13, 22)
 LANES = 128
 MESH = pl.DeviceIdType.MESH
 F32 = jnp.float32
@@ -33,6 +35,23 @@
     nrow,
     ncol,
     pair,
+    direct,
+    jump_hbm,
+    external_hbm,
+    cohesive_hbm,
+    bond_hbm,
+    load_hbm,
+    radius_hbm,
+    coupling_hbm,
+    steps_hbm,
+    points_hbm,
+    stiffness_hbm,
+    state_hbm,
+    history_hbm,
+    new_jump_ref,
+    new_load_ref,
+    new_state_ref,
+    new_history_ref,
     jump_ref,
     external_ref,
     cohesive_ref,
@@ -42,13 +61,6 @@
     coupling_ref,
     steps_ref,
     points_ref,
-    stiffness_hbm,
-    state_hbm,
-    history_hbm,
-    new_jump_ref,
-    new_load_ref,
-    new_state_ref,
-    new_history_ref,
     stiff,
     state,
     history,
@@ -84,25 +96,53 @@
     width = devices * padded
     bits = devices.bit_length() - 1
 
-    fetch = [
-        pltpu.make_async_copy(history_hbm, history, local_sems.at[0]),
-        pltpu.make_async_copy(stiffness_hbm, stiff, local_sems.at[1]),
-        pltpu.make_async_copy(state_hbm, state, local_sems.at[2]),
-    ]
-    for copy in fetch:
-        copy.start()
+    half = devices // 2
+    side = lax.div(row, nrow // 2)
+
+    names = (
+        (steps_hbm, steps_ref),
+        (jump_hbm, jump_ref),
+        (bond_hbm, bond_ref),
+        (points_hbm, points_ref),
+        (coupling_hbm, coupling_ref),
+        (history_hbm, history),
+        (stiffness_hbm, stiff),
+        (state_hbm, state),
+        (external_hbm, external_ref),
+        (cohesive_hbm, cohesive_ref),
+        (load_hbm, load_ref),
+        (radius_hbm, radius_ref),
+    )
+    fetch = []
+    for index, (source, target) in enumerate(names):
+        fetch.append(pltpu.make_async_copy(source, target, local_sems.at[index]))
+        fetch[-1].start()
+
+    def locate(p):
+        return {"row": lax.div(p, ncol), "col": lax.rem(p, ncol)}
 
     def peer(k):
         p = lax.rem(here + k, devices)
-        return {"row": lax.div(p, ncol), "col": lax.rem(p, ncol)}, p
+        return locate(p), p
 
     x_in[...] = jnp.zeros_like(x_in)
     y_in[...] = jnp.zeros_like(y_in)
+
+    barrier = pltpu.get_barrier_semaphore()
+
+    def greet(k, carry):
+        device, _ = peer(k)
+        pl.semaphore_signal(barrier, inc=1, device_id=device, device_id_type=MESH)
+        return carry
+
+    lax.fori_loop(1, devices, greet, 0)
+
     if pair < padded:
         blank = jnp.zeros((devices, padded - pair, cells), F32)
         in_history[:, pair:, :] = blank
         in_state[:, pair:, :] = blank
 
+    fetch[0].wait()
     steps_row = steps_ref[...]
     live_row = (steps_row > 0).astype(F32)
     count_out[...] = jnp.broadcast_to(jnp.sum(live_row, axis=1, keepdims=True), count_out.shape)
@@ -111,15 +151,19 @@
     line = iota((X, Y), 0)
 
     def stage(phase, fields):
-        right = jnp.zeros((X, Y), F32)
-        left = jnp.zeros((X, Y), F32)
+        edges = jnp.zeros((X, Y), F32)
         for c, (x_field, y_field) in enumerate(fields):
             x_out[phase, 0, c : c + 1, :] = x_field[X - 1 : X, :]
             x_out[phase, 1, c : c + 1, :] = x_field[0:1, :]
-            right = jnp.where(lane == c, pltpu.roll(y_field, (c + 1) % Y, 1), right)
-            left = jnp.where(lane == c, pltpu.roll(y_field, c, 1), left)
-        y_out[phase, 0] = right
-        y_out[phase, 1] = left
+            edges = jnp.where(lane == c, pltpu.roll(y_field, (c + 1) % Y, 1), edges)
+            edges = jnp.where(lane == c + 8, pltpu.roll(y_field, c + 8, 1), edges)
+        turned_edges = jnp.concatenate([edges, jnp.zeros((Y - X, Y), F32)], axis=0).T
+        y_out[phase, 0] = turned_edges[0:8, :]
+        y_out[phase, 1] = turned_edges[8:16, :]
+
+    def edges_of(phase):
+        both = [y_in[phase, 0], y_in[phase, 1], jnp.zeros((Y - 16, Y), F32)]
+        return jnp.concatenate(both, axis=0).T[:X, :]
 
     def halo_copies(phase):
         plan = (
@@ -153,17 +197,20 @@
         for copy, sends, gets in halo_copies(phase):
             pl.when(sends)(copy.wait_send)
 
+    def send(source, target, kind, device):
+        pltpu.make_async_remote_copy(
+            src_ref=source,
+            dst_ref=target,
+            send_sem=all_send.at[kind],
+            recv_sem=all_recv.at[kind],
+            device_id=device,
+            device_id_type=MESH,
+        ).start()
+
     def spread(source_of, target, kind, first, last):
         def one(k, carry):
             device, p = peer(k)
-            pltpu.make_async_remote_copy(
-                src_ref=source_of(p),
-                dst_ref=target,
-                send_sem=all_send.at[kind],
-                recv_sem=all_recv.at[kind],
-                device_id=device,
-                device_id_type=MESH,
-            ).start()
+            send(source_of(p), target, kind, device)
             return carry
 
         lax.fori_loop(first, last, one, 0)
@@ -171,25 +218,57 @@
     def spread_wait(buffer, sem):
         pltpu.make_async_copy(buffer, buffer, sem).wait()
 
+    direct_part = pl.ds(0, direct)
+    shared_part = pl.ds(direct, pair - direct)
+
+    def send_shared(out, inside, kind):
+        if direct == pair:
+            return
+
+        def one(k, carry):
+            p = side * half + lax.rem(lax.rem(here, half) + k, half)
+            send(out.at[p, shared_part], inside.at[here, shared_part], kind, locate(p))
+            return carry
+
+        lax.fori_loop(1, half, one, 0)
+
+    def send_direct(out, inside, kind, first, last):
+        spread(
+            lambda p: out.at[p, direct_part], inside.at[here, direct_part], kind, first, last
+        )
+
+    def forward(inside, kind):
+        if direct == pair:
+            return
+        spread_wait(inside.at[pl.ds(0, half - 1), shared_part], all_recv.at[kind])
+        mine = inside.at[pl.ds(side * half, half), shared_part]
+        send(mine, mine, kind + 2, locate(lax.rem(here + half, devices)))
+
+    def rows_wait(inside, kind):
+        spread_wait(inside.at[pl.ds(0, devices - 1), direct_part], all_recv.at[kind + 1])
+        if direct < pair:
+            spread_wait(inside.at[pl.ds(0, half), shared_part], all_recv.at[kind + 2])
+
+    def sends_wait(inside, kind):
+        spread_wait(inside.at[pl.ds(0, devices - 1), direct_part], all_send.at[kind + 1])
+        if direct < pair:
+            spread_wait(inside.at[pl.ds(0, half - 1), shared_part], all_send.at[kind])
+            spread_wait(inside.at[pl.ds(0, half), shared_part], all_send.at[kind + 2])
+
+    fetch[1].wait()
+    fetch[2].wait()
     bond_x = 0.25 + 0.75 * bond_ref[0].astype(F32)
     bond_y = 0.25 + 0.75 * bond_ref[1].astype(F32)
     jump = [jump_ref[c] for c in range(3)]
     stage(0, [(jump[c], jump[c]) for c in range(3)] + [(bond_x, bond_y)])
 
-    barrier = pltpu.get_barrier_semaphore()
-
-    def greet(k, carry):
-        device, _ = peer(k)
-        pl.semaphore_signal(barrier, inc=1, device_id=device, device_id_type=MESH)
-        return carry
-
-    lax.fori_loop(1, devices, greet, 0)
     pl.semaphore_wait(barrier, devices - 1)
 
     count_in[pl.ds(here, 1)] = count_out[...][None]
     spread(lambda p: count_out, count_in.at[here], 0, 1, devices)
     halo_start(0)
 
+    fetch[3].wait()
     slot_line = iota((slots, slots), 0)
     slot_lane = iota((slots, slots), 1)
 
@@ -206,6 +285,7 @@
     at_x = (iota((slots, X), 1) == px_col).astype(F32).astype(BF16)
     at_y = (iota((slots, Y), 1) == py_col).astype(F32)
     at_x_turned = (iota((X, slots), 0) == px_row).astype(F32).astype(BF16)
+    fetch[4].wait()
     drive = []
     for c in range(3):
         lines = picked(at_x, jump[c])
@@ -217,56 +297,13 @@
         load[:, part] = total + drive[2] * coupling_ref[2:3, part]
     rank_row = jnp.sum(jnp.where(slot_line < slot_lane, live_col, 0.0), axis=0, keepdims=True)
 
-    fetch[0].wait()
+    fetch[5].wait()
     for start in range(0, cells, TILE):
         part = slice(start, start + TILE)
         damage[:, part] = jnp.exp(-history[:, part])
 
-    spread_wait(count_in.at[pl.ds(0, devices - 1)], all_recv.at[0])
-    counts = jnp.max(count_in[...], axis=1)
-    device_line = iota((devices, LANES), 0)
-    device_lane = iota((devices, LANES), 1)
-    starts = jnp.sum(jnp.where(device_line < device_lane, counts, 0.0), axis=0, keepdims=True)
-    ends = jnp.sum(jnp.where(device_line <= device_lane, counts, 0.0), axis=0, keepdims=True)
-    my_start = jnp.sum(jnp.where(device_line < here, counts, 0.0), axis=0, keepdims=True)[:, :1]
-    my_start = my_start.astype(jnp.int32)
-
-    def place(rank, first):
-        pairs = lax.shift_right_logical(rank, 1) - lax.shift_right_logical(first, 1)
-        return 2 * lax.shift_right_logical(pairs, bits) + (rank & 1)
-
-    ranks = rank_row.astype(jnp.int32) + my_start
-    home = lax.shift_right_logical(ranks, 1) & (devices - 1)
-    leaves = jnp.where(steps_row > 0, home * padded + place(ranks, my_start), -1)
-    leaving = (iota((width, slots), 0) == leaves).astype(F32).astype(BF16)
-
-    wanted_slot = iota((new_cap, LANES), 0)
-    wanted = 2 * (here + devices * lax.shift_right_logical(wanted_slot, 1)) + (wanted_slot & 1)
-    wanted_lane = iota((new_cap, LANES), 1)
-    wanted_float = wanted.astype(F32)
-    hit = (starts <= wanted_float) & (wanted_float < ends) & (wanted_lane < devices)
-    valid = jnp.sum(jnp.where(hit, 1.0, 0.0), axis=1, keepdims=True)
-    from_start = jnp.sum(jnp.where(hit, starts, 0.0), axis=1, keepdims=True).astype(jnp.int32)
-    source = jnp.sum(jnp.where(hit, wanted_lane.astype(F32), 0.0), axis=1, keepdims=True)
-    arrives = source.astype(jnp.int32) * padded + place(wanted[:, :1], from_start)
-    arrives = jnp.where(valid > 0.0, arrives, -1)
-    coming = (iota((new_cap, width), 1) == arrives).astype(F32).astype(BF16)
-
-    def gather_out(values, out, inside):
-        for start in range(0, cells, TILE):
-            part = slice(start, start + TILE)
-            rows = picked(leaving, values[:, part])
-            out[:, :, part] = rows.reshape(devices, padded, TILE)
-        inside[pl.ds(here, 1)] = out[pl.ds(here, 1)]
-
-    gather_out(history, out_history, in_history)
-    row_part = pl.ds(0, pair)
-    spread(
-        lambda p: out_history.at[p, row_part], in_history.at[here, row_part], 1, 1, devices
-    )
-
-    fetch[1].wait()
-    fetch[2].wait()
+    fetch[6].wait()
+    fetch[7].wait()
     tile_eye = iota((TILE, TILE), 0) == iota((TILE, TILE), 1)
     for start in range(0, cells, TILE):
         part = slice(start, start + TILE)
@@ -290,22 +327,67 @@
             rounded[1 - now, :, part] = current.astype(BF16)
         return carry
 
-    lax.fori_loop(0, MAX_STEPS, advance, 0)
+    lax.fori_loop(0, EARLY, advance, 0)
+
+    spread_wait(count_in.at[pl.ds(0, devices - 1)], all_recv.at[0])
+    counts = count_in[:, 0, :]
+    device_line = iota((devices, LANES), 0)
+    device_lane = iota((devices, LANES), 1)
+    starts = jnp.sum(jnp.where(device_line < device_lane, counts, 0.0), axis=0, keepdims=True)
+    ends = jnp.sum(jnp.where(device_line <= device_lane, counts, 0.0), axis=0, keepdims=True)
+    my_start = jnp.sum(jnp.where(device_line < here, counts, 0.0), axis=0, keepdims=True)[:, :1]
+    my_start = my_start.astype(jnp.int32)
+
+    def place(rank, first):
+        pairs = lax.shift_right_logical(rank, 1) - lax.shift_right_logical(first, 1)
+        spot = 2 * lax.shift_right_logical(pairs, bits) + (rank & 1)
+        if direct == pair:
+            return spot
+        spot = spot - jnp.where((pairs & (devices - 1)) == 0, first & 1, 0)
+        return jnp.where(spot < direct, spot, direct + (rank & 1))
+
+    ranks = rank_row.astype(jnp.int32) + my_start
+    home = lax.shift_right_logical(ranks, 1) & (devices - 1)
+    spots = place(ranks, my_start)
+    if direct < pair:
+        home = jnp.where(spots < direct, home, (home & (half - 1)) + side * half)
+    leaves = jnp.where(steps_row > 0, home * padded + spots, -1)
+    leaving = (iota((width, slots), 0) == leaves).astype(F32).astype(BF16)
+
+    wanted_slot = iota((new_cap, LANES), 0)
+    wanted = 2 * (here + devices * lax.shift_right_logical(wanted_slot, 1)) + (wanted_slot & 1)
+    wanted_lane = iota((new_cap, LANES), 1)
+    wanted_float = wanted.astype(F32)
+    hit = (starts <= wanted_float) & (wanted_float < ends) & (wanted_lane < devices)
+    valid = jnp.sum(jnp.where(hit, 1.0, 0.0), axis=1, keepdims=True)
+    from_start = jnp.sum(jnp.where(hit, starts, 0.0), axis=1, keepdims=True).astype(jnp.int32)
+    source = jnp.sum(jnp.where(hit, wanted_lane.astype(F32), 0.0), axis=1, keepdims=True)
+    arrives = source.astype(jnp.int32) * padded + place(wanted[:, :1], from_start)
+    arrives = jnp.where(valid > 0.0, arrives, -1)
+    coming = (iota((new_cap, width), 1) == arrives).astype(F32).astype(BF16)
+
+    def gather_out(values, out, inside):
+        for start in range(0, cells, TILE):
+            part = slice(start, start + TILE)
+            rows = picked(leaving, values[:, part])
+            out[:, :, part] = rows.reshape(devices, padded, TILE)
+        inside[pl.ds(here, 1)] = out[pl.ds(here, 1)]
+
+    gather_out(history, out_history, in_history)
+    send_shared(out_history, in_history, 1)
+    send_direct(out_history, in_history, 2, 1, devices)
+
+    lax.fori_loop(EARLY, MAX_STEPS, advance, 0)
 
     others = devices - 1
-    bounds = [1] + [1 + others * s // 20 for s in (4, 10, 15)] + [devices]
+    bounds = [1] + [1 + others * s // 31 for s in CHUNKS] + [devices]
+
+    gather_out(state, out_state, in_state)
 
     def send_state(step):
-        spread(
-            lambda p: out_state.at[p, row_part],
-            in_state.at[here, row_part],
-            2,
-            bounds[step],
-            bounds[step + 1],
-        )
-
-    gather_out(state, out_state, in_state)
-    send_state(0)
+        if step == 0:
+            send_shared(out_state, in_state, 4)
+        send_direct(out_state, in_state, 5, bounds[step], bounds[step + 1])
 
     first_sum = jnp.zeros((slots, 16), F32)
     second_sum = jnp.zeros((slots, 16), F32)
@@ -347,6 +429,8 @@
     tangent = [put(second_sum[:, c : c + 1]) for c in range(6)]
 
     halo_wait(0)
+    for copy in fetch[8:]:
+        copy.wait()
 
     def before_x(phase, field, c):
         return jnp.where(line == 0, x_in[phase, 0, c : c + 1, :], pltpu.roll(field, 1, 0))
@@ -354,33 +438,35 @@
     def after_x(phase, field, c):
         return jnp.where(line == X - 1, x_in[phase, 1, c : c + 1, :], pltpu.roll(field, X - 1, 0))
 
-    def before_y(phase, field, c):
-        edge = pltpu.roll(y_in[phase, 0], (Y - c) % Y, 1)
+    def before_y(edges, field, c):
+        edge = pltpu.roll(edges, (Y - c) % Y, 1)
         return jnp.where(lane == 0, edge, pltpu.roll(field, 1, 1))
 
-    def after_y(phase, field, c):
-        edge = pltpu.roll(y_in[phase, 1], Y - 1 - c, 1)
+    def after_y(edges, field, c):
+        edge = pltpu.roll(edges, Y - 9 - c, 1)
         return jnp.where(lane == Y - 1, edge, pltpu.roll(field, Y - 1, 1))
 
     low_x = before_x(0, bond_x, 3)
-    low_y = before_y(0, bond_y, 3)
-
-    def neighbours(phase, field, c):
+    first_edges = edges_of(0)
+    low_y = before_y(first_edges, bond_y, 3)
+
+    def neighbours(phase, edges, field, c):
         return (
             bond_x * after_x(phase, field, c)
             + low_x * before_x(phase, field, c)
-            + bond_y * after_y(phase, field, c)
-            + low_y * before_y(phase, field, c)
+            + bond_y * after_y(edges, field, c)
+            + low_y * before_y(edges, field, c)
         )
 
     scale = bond_x + low_x + bond_y + low_y + (1.0 - soft) * cohesive_ref[...]
+    load_factor = load_ref[...]
     terms = []
     for c in range(3):
         residual = (
             scale * jump[c]
-            - neighbours(0, jump[c], c)
+            - neighbours(0, first_edges, jump[c], c)
             + rve_traction[c]
-            - load_ref[0] * external_ref[c]
+            - load_factor * external_ref[c]
         )
         terms.append(-residual)
     for c in range(3):
@@ -410,15 +496,20 @@
         phase = sweep + 1
         stage(phase, [(v, v) for v in iterate])
         halo_start(phase)
-        send_state(sweep + 1)
         if sweep == 0:
-            spread_wait(in_history.at[peers, row_part], all_recv.at[1])
+            forward(in_history, 1)
+        send_state(sweep)
+        if sweep == 1:
+            rows_wait(in_history, 1)
             for start in range(0, cells, TILE):
                 part = slice(start, start + TILE)
                 kept = picked(coming, in_history[:, :, part].reshape(width, TILE))
                 new_history_ref[:, part] = kept
+        if sweep == 2:
+            forward(in_state, 4)
         halo_wait(phase)
-        iterate = solve_both([terms[c] + neighbours(phase, iterate[c], c) for c in range(6)])
+        edges = edges_of(phase)
+        iterate = solve_both([terms[c] + neighbours(phase, edges, iterate[c], c) for c in range(6)])
     correction, direction = iterate[:3], iterate[3:]
 
     def total_of(fields):
@@ -426,22 +517,25 @@
 
     cross_row = total_of([correction[c] * direction[c] for c in range(3)])
     square_row = total_of([direction[c] * direction[c] for c in range(3)])
-    sum_out[...] = jnp.where(iota((8, Y), 0) == 0, cross_row, square_row)
+    own_cross = jnp.sum(cross_row, axis=1, keepdims=True)
+    own_square = jnp.sum(square_row, axis=1, keepdims=True)
+    sum_out[...] = jnp.where(iota((1, Y), 1) == 0, own_cross, own_square)
     sum_in[pl.ds(here, 1)] = sum_out[...][None]
-    spread(lambda p: sum_out, sum_in.at[here], 3, 1, devices)
-    spread_wait(sum_in.at[pl.ds(0, devices - 1)], all_recv.at[3])
+    spread(lambda p: sum_out, sum_in.at[here], 7, 1, devices)
+    send_state(SWEEPS)
+    spread_wait(sum_in.at[pl.ds(0, devices - 1)], all_recv.at[7])
     sums = jnp.sum(sum_in[...], axis=0)
-    cross = jnp.sum(sums[0:1, :], axis=1, keepdims=True)
-    square = jnp.sum(sums[1:2, :], axis=1, keepdims=True)
+    cross = sums[:, 0:1]
+    square = sums[:, 1:2]
     entries = 3.0 * X * Y * devices
     shifted = square + 0.25 * entries
     root = jnp.sqrt(shifted) * (entries**0.5)
-    increment = (radius_ref[0] * root - cross) / shifted
+    increment = (radius_ref[...] * root - cross) / shifted
     for c in range(3):
         new_jump_ref[c] = jump[c] + correction[c] + increment * direction[c]
-    new_load_ref[...] = load_ref[0] + increment
-
-    spread_wait(in_state.at[peers, row_part], all_recv.at[2])
+    new_load_ref[...] = load_factor + increment
+
+    rows_wait(in_state, 4)
     for start in range(0, cells, TILE):
         part = slice(start, start + TILE)
         moved = picked(coming, in_state[:, :, part].reshape(width, TILE))
@@ -451,9 +545,9 @@
     for phase in range(SWEEPS + 1):
         halo_wait_sends(phase)
     spread_wait(count_in.at[peers], all_send.at[0])
-    spread_wait(out_history.at[peers, row_part], all_send.at[1])
-    spread_wait(out_state.at[peers, row_part], all_send.at[2])
-    spread_wait(sum_in.at[peers], all_send.at[3])
+    sends_wait(out_history, 1)
+    sends_wait(out_state, 4)
+    spread_wait(sum_in.at[peers], all_send.at[7])
 
 
 def on_device(
@@ -478,20 +572,30 @@
     pair = 2 * ((slots + 2 * devices + 1) // (2 * devices))
     padded = 8 * ((pair + 7) // 8)
     phases = SWEEPS + 1
+    shares = pair > 2 and nrow % 2 == 0 and slots <= (pair - 1) * devices
+    direct = pair - 2 if shares else pair
     vmem = pl.BlockSpec(memory_space=pltpu.VMEM)
-    smem = pl.BlockSpec(memory_space=pltpu.SMEM)
-    hbm = pl.BlockSpec(memory_space=pl.ANY)
+    hbm = pl.BlockSpec(memory_space=pltpu.HBM)
     new_jump, new_load, new_state, new_history = pl.pallas_call(
-        functools.partial(body, nrow, ncol, pair),
+        functools.partial(body, nrow, ncol, pair, direct),
         out_shape=(
             jax.ShapeDtypeStruct(jump.shape, F32),
             jax.ShapeDtypeStruct((1, 1), F32),
             jax.ShapeDtypeStruct((new_cap, cells), F32),
             jax.ShapeDtypeStruct((new_cap, cells), F32),
         ),
-        in_specs=[vmem] * 4 + [smem] * 2 + [vmem] * 3 + [hbm] * 3,
+        in_specs=[hbm] * 12,
         out_specs=(vmem,) * 4,
         scratch_shapes=[
+            pltpu.VMEM(jump.shape, F32),
+            pltpu.VMEM(external.shape, F32),
+            pltpu.VMEM(cohesive.shape, F32),
+            pltpu.VMEM(bond_mask.shape, jnp.int32),
+            pltpu.VMEM((1, 1), F32),
+            pltpu.VMEM((1, 1), F32),
+            pltpu.VMEM(coupling.shape, F32),
+            pltpu.VMEM((1, slots), jnp.int32),
+            pltpu.VMEM((1, slots), jnp.int32),
             pltpu.VMEM((cells, cells), BF16),
             pltpu.VMEM((slots, cells), F32),
             pltpu.VMEM((slots, cells), F32),
@@ -499,23 +603,23 @@
             pltpu.VMEM((slots, cells), F32),
             pltpu.VMEM((2, slots, cells), BF16),
             pltpu.VMEM((1, cells), F32),
-            pltpu.VMEM((8, LANES), F32),
-            pltpu.VMEM((devices, 8, LANES), F32),
-            pltpu.VMEM((8, Y), F32),
-            pltpu.VMEM((devices, 8, Y), F32),
+            pltpu.VMEM((1, LANES), F32),
+            pltpu.VMEM((devices, 1, LANES), F32),
+            pltpu.VMEM((1, Y), F32),
+            pltpu.VMEM((devices, 1, Y), F32),
             pltpu.VMEM((phases, 2, 8, Y), F32),
             pltpu.VMEM((phases, 2, 8, Y), F32),
-            pltpu.VMEM((phases, 2, X, Y), F32),
-            pltpu.VMEM((phases, 2, X, Y), F32),
+            pltpu.VMEM((phases, 2, 8, Y), F32),
+            pltpu.VMEM((phases, 2, 8, Y), F32),
             pltpu.VMEM((devices, padded, cells), F32),
             pltpu.VMEM((devices, padded, cells), F32),
             pltpu.VMEM((devices, padded, cells), F32),
             pltpu.VMEM((devices, padded, cells), F32),
-            pltpu.SemaphoreType.DMA((3,)),
+            pltpu.SemaphoreType.DMA((12,)),
             pltpu.SemaphoreType.DMA((phases, 4)),
             pltpu.SemaphoreType.DMA((phases, 4)),
-            pltpu.SemaphoreType.DMA((4,)),
-            pltpu.SemaphoreType.DMA((4,)),
+            pltpu.SemaphoreType.DMA((8,)),
+            pltpu.SemaphoreType.DMA((8,)),
         ],
         compiler_params=pltpu.CompilerParams(
             collective_id=0, has_side_effects=True, vmem_limit_bytes=60 * 1024 * 1024
@@ -525,8 +629,8 @@
         external,
         cohesive,
         bond_mask,
-        load_factor,
-        arc_radius,
+        load_factor.reshape(1, 1),
+        arc_radius.reshape(1, 1),
         coupling,
         newton_steps.reshape(1, slots),
         point_ids.reshape(1, slots),

time: 83.7 us -> 67.8 us (0.81)
  Pallas kernels: 74.5 us -> 58.6 us
    pallas_call x1, Pallas kernels: 74.5 us -> 58.6 us  [on_device(): pl.pallas_call(functools.partial(body, nrow, ncol, pair, direct), out_sha...]
where the time goes in v1:
time: 67.8 us; the launch traced here: 67.5 us
  Pallas kernels  58.6 us (86%)
  local copies, waits for them, and re-layouts  5.23 us (8%)
  between operations  3.7 us (5%)
    pallas_call x1, Pallas kernels, on_device(): pl.pallas_call(functools.partial(body, nrow, ncol, pair, direct), out_sha...  58.6 us
    unnamed x3, local copies, waits for them, and re-layouts  5.23 us

profile of v1, /device:TPU:0, one launch (start us, length us, event | category | flops | bytes accessed | tf_op | source)
XLA Modules:
  0.0 67.5 jit_solution(12867916176402338024)
XLA Ops:
  1.9 58.6 %shard_map.147 = (f32[3,64,128]{2,1,0:T(8,128)}, f32[1,1]{1,0:T(1,128)}, f32[80,1536]{1,0:T(8,128)}, f32[80,1536]{1,0:T(8,128)}) custom-call(f32[3,64,128]{2,1,0:T(8,128)} %jump_hbm.1, f32[3,64,128]{2,1,0:T(8,128)} %external_hbm.1, f32[64,128]{1,0:T(8,128)} %cohesive_hbm.1, s32[2,64,128]{2,1,0:T(8,128)} %bond_hbm.1, f32[1,1]{1,0:T(1,128)} %bitcast.5.load_hbm, ...), custom_call_target="tpu_custom_call" | custom-call | tf_op jit(solution)/shard_map/pallas_call | solution.py:579
  60.5 1.5 %copy.22 = f32[3,64,128]{2,1,0:T(8,128)} copy(f32[3,64,128]{2,1,0:T(8,128)} %get-tuple-element.16) | data formatting | bytes 196608
  62.7 1.8 %copy.24 = f32[80,1536]{1,0:T(8,128)} copy(f32[80,1536]{1,0:T(8,128)} %get-tuple-element.18) | data formatting | bytes 983040
  64.6 1.8 %copy.25 = f32[80,1536]{1,0:T(8,128)} copy(f32[80,1536]{1,0:T(8,128)} %get-tuple-element.19) | data formatting | bytes 983040

commit v2 on v1

--- a/solution.py
+++ b/solution.py
@@ -11,6 +11,7 @@
 SWEEPS = 3
 TILE = 256
 EARLY = 1
+GRANT = 60 * 1024 * 1024
 CHUNKS = (5, 13, 22)
 LANES = 128
 MESH = pl.DeviceIdType.MESH
@@ -459,7 +460,7 @@
         )
 
     scale = bond_x + low_x + bond_y + low_y + (1.0 - soft) * cohesive_ref[...]
-    load_factor = load_ref[...]
+    load_factor = load_ref[0]
     terms = []
     for c in range(3):
         residual = (
@@ -530,7 +531,7 @@
     entries = 3.0 * X * Y * devices
     shifted = square + 0.25 * entries
     root = jnp.sqrt(shifted) * (entries**0.5)
-    increment = (radius_ref[...] * root - cross) / shifted
+    increment = (radius_ref[0] * root - cross) / shifted
     for c in range(3):
         new_jump_ref[c] = jump[c] + correction[c] + increment * direction[c]
     new_load_ref[...] = load_factor + increment
@@ -540,7 +541,6 @@
         part = slice(start, start + TILE)
         moved = picked(coming, in_state[:, :, part].reshape(width, TILE))
         new_state_ref[:, part] = moved
-        new_history_ref[:, part] = jnp.maximum(new_history_ref[:, part], jnp.abs(moved))
 
     for phase in range(SWEEPS + 1):
         halo_wait_sends(phase)
@@ -548,6 +548,14 @@
     sends_wait(out_history, 1)
     sends_wait(out_state, 4)
     spread_wait(sum_in.at[peers], all_send.at[7])
+
+
+def finish(jump_ref, load_ref, state_ref, history_ref, *outs):
+    new_jump_ref, new_load_ref, new_state_ref, new_history_ref = outs
+    new_jump_ref[...] = jump_ref[...]
+    new_load_ref[...] = load_ref[...]
+    new_state_ref[...] = state_ref[...]
+    new_history_ref[...] = jnp.maximum(history_ref[...], jnp.abs(state_ref[...]))
 
 
 def on_device(
@@ -574,16 +582,17 @@
     phases = SWEEPS + 1
     shares = pair > 2 and nrow % 2 == 0 and slots <= (pair - 1) * devices
     direct = pair - 2 if shares else pair
+    out_shape = (
+        jax.ShapeDtypeStruct(jump.shape, F32),
+        jax.ShapeDtypeStruct((1, 1), F32),
+        jax.ShapeDtypeStruct((new_cap, cells), F32),
+        jax.ShapeDtypeStruct((new_cap, cells), F32),
+    )
     vmem = pl.BlockSpec(memory_space=pltpu.VMEM)
     hbm = pl.BlockSpec(memory_space=pltpu.HBM)
-    new_jump, new_load, new_state, new_history = pl.pallas_call(
+    results = pl.pallas_call(
         functools.partial(body, nrow, ncol, pair, direct),
-        out_shape=(
-            jax.ShapeDtypeStruct(jump.shape, F32),
-            jax.ShapeDtypeStruct((1, 1), F32),
-            jax.ShapeDtypeStruct((new_cap, cells), F32),
-            jax.ShapeDtypeStruct((new_cap, cells), F32),
-        ),
+        out_shape=out_shape,
         in_specs=[hbm] * 12,
         out_specs=(vmem,) * 4,
         scratch_shapes=[
@@ -591,8 +600,8 @@
             pltpu.VMEM(external.shape, F32),
             pltpu.VMEM(cohesive.shape, F32),
             pltpu.VMEM(bond_mask.shape, jnp.int32),
-            pltpu.VMEM((1, 1), F32),
-            pltpu.VMEM((1, 1), F32),
+            pltpu.SMEM((1,), F32),
+            pltpu.SMEM((1,), F32),
             pltpu.VMEM(coupling.shape, F32),
             pltpu.VMEM((1, slots), jnp.int32),
             pltpu.VMEM((1, slots), jnp.int32),
@@ -622,15 +631,15 @@
             pltpu.SemaphoreType.DMA((8,)),
         ],
         compiler_params=pltpu.CompilerParams(
-            collective_id=0, has_side_effects=True, vmem_limit_bytes=60 * 1024 * 1024
+            collective_id=0, has_side_effects=True, vmem_limit_bytes=GRANT
         ),
     )(
         jump,
         external,
         cohesive,
         bond_mask,
-        load_factor.reshape(1, 1),
-        arc_radius.reshape(1, 1),
+        load_factor,
+        arc_radius,
         coupling,
         newton_steps.reshape(1, slots),
         point_ids.reshape(1, slots),
@@ -638,6 +647,13 @@
         old_state,
         old_history,
     )
+    new_jump, new_load, new_state, new_history = pl.pallas_call(
+        finish,
+        out_shape=out_shape,
+        in_specs=[vmem] * 4,
+        out_specs=(vmem,) * 4,
+        compiler_params=pltpu.CompilerParams(vmem_limit_bytes=GRANT),
+    )(*results)
     return new_jump, new_load.reshape(1), new_state, new_history
 
 

time: 67.8 us -> 63.5 us (0.937)
  local copies, waits for them, and re-layouts: 5.23 us -> 0 us
  Pallas kernels: 58.6 us -> 61.4 us
  between operations: 3.7 us -> 1.93 us
    unnamed x3 -> x0, local copies, waits for them, and re-layouts: 5.23 us -> none
    pallas_call x0 -> x1, Pallas kernels: none -> 2.8 us  [on_device(): pl.pallas_call(finish, out_shape=out_shape, in_specs=[vmem] * 4, out_spec...]
where the time goes in v2:
time: 63.5 us; the launch traced here: 63.4 us
  Pallas kernels  61.4 us (97%)
  between operations  1.93 us (3%)
    pallas_call x1, Pallas kernels, on_device(): pl.pallas_call(functools.partial(body, nrow, ncol, pair, direct), out_sha...  58.6 us
    pallas_call x1, Pallas kernels, on_device(): pl.pallas_call(finish, out_shape=out_shape, in_specs=[vmem] * 4, out_spec...  2.8 us

profile of v2, /device:TPU:0, one launch (start us, length us, event | category | flops | bytes accessed | tf_op | source)
XLA Modules:
  0.0 63.4 jit_solution(17868826721724580925)
XLA Ops:
  1.9 58.6 %shard_map.147 = (f32[3,64,128]{2,1,0:T(8,128)}, f32[1,1]{1,0:T(1,128)}, f32[80,1536]{1,0:T(8,128)}, f32[80,1536]{1,0:T(8,128)}) custom-call(f32[3,64,128]{2,1,0:T(8,128)} %jump_hbm.1, f32[3,64,128]{2,1,0:T(8,128)} %external_hbm.1, f32[64,128]{1,0:T(8,128)} %cohesive_hbm.1, s32[2,64,128]{2,1,0:T(8,128)} %bond_hbm.1, f32[1]{0:T(128)S(6)} %copy.16.load_hbm, ...), custom_call_target="tpu_custom_call" | custom-call | tf_op jit(solution)/shard_map/pallas_call | solution.py:593
  60.6 2.8 %shard_map.148 = (f32[3,64,128]{2,1,0:T(8,128)}, f32[1,1]{1,0:T(1,128)}, f32[80,1536]{1,0:T(8,128)}, f32[80,1536]{1,0:T(8,128)}) custom-call(f32[3,64,128]{2,1,0:T(8,128)} %get-tuple-element.12.jump_ref, f32[1,1]{1,0:T(1,128)} %get-tuple-element.13.load_ref, f32[80,1536]{1,0:T(8,128)} %get-tuple-element.14.state_ref, f32[80,1536]{1,0:T(8,128)} %get-tuple-element.15.history_ref), custom_call_target="tpu_custom_call" | custom-call | tf_op jit(solution)/shard_map/pallas_call | solution.py:650

commit v3 on v2

--- a/solution.py
+++ b/solution.py
@@ -10,9 +10,10 @@
 MAX_STEPS = 9
 SWEEPS = 3
 TILE = 256
+WIDE = 768
 EARLY = 1
 GRANT = 60 * 1024 * 1024
-CHUNKS = (5, 13, 22)
+CHUNKS = (4, 11, 19)
 LANES = 128
 MESH = pl.DeviceIdType.MESH
 F32 = jnp.float32
@@ -23,13 +24,21 @@
     return lax.broadcasted_iota(jnp.int32, shape, dim)
 
 
-def picked(onehot, values):
+def pieces_of(values):
     high = values.astype(BF16)
     rest = values - high.astype(F32)
     middle = rest.astype(BF16)
     low = (rest - middle.astype(F32)).astype(BF16)
+    return high, middle, low
+
+
+def joined(onehot, pieces):
     dot = functools.partial(jnp.dot, preferred_element_type=F32)
-    return dot(onehot, high) + dot(onehot, middle) + dot(onehot, low)
+    return dot(onehot, pieces[0]) + dot(onehot, pieces[1]) + dot(onehot, pieces[2])
+
+
+def picked(onehot, values):
+    return joined(onehot, pieces_of(values))
 
 
 def body(
@@ -49,10 +58,16 @@
     stiffness_hbm,
     state_hbm,
     history_hbm,
+    new_jump_hbm,
+    new_load_hbm,
+    coming_hbm,
+    kept_hbm,
+    in_state,
     new_jump_ref,
     new_load_ref,
-    new_state_ref,
-    new_history_ref,
+    coming_ref,
+    kept_ref,
+    pieces,
     jump_ref,
     external_ref,
     cohesive_ref,
@@ -80,8 +95,8 @@
     out_history,
     in_history,
     out_state,
-    in_state,
     local_sems,
+    result_sems,
     halo_send,
     halo_recv,
     all_send,
@@ -92,7 +107,7 @@
     here = row * ncol + col
     slots, cells = state.shape
     X, Y = cohesive_ref.shape
-    new_cap = new_state_ref.shape[0]
+    new_cap = kept_ref.shape[0]
     padded = out_history.shape[1]
     width = devices * padded
     bits = devices.bit_length() - 1
@@ -117,7 +132,7 @@
     fetch = []
     for index, (source, target) in enumerate(names):
         fetch.append(pltpu.make_async_copy(source, target, local_sems.at[index]))
-        fetch[-1].start()
+    fetch[0].start()
 
     def locate(p):
         return {"row": lax.div(p, ncol), "col": lax.rem(p, ncol)}
@@ -137,11 +152,12 @@
         return carry
 
     lax.fori_loop(1, devices, greet, 0)
+    for copy in fetch[1:]:
+        copy.start()
 
     if pair < padded:
         blank = jnp.zeros((devices, padded - pair, cells), F32)
         in_history[:, pair:, :] = blank
-        in_state[:, pair:, :] = blank
 
     fetch[0].wait()
     steps_row = steps_ref[...]
@@ -238,10 +254,10 @@
             lambda p: out.at[p, direct_part], inside.at[here, direct_part], kind, first, last
         )
 
-    def forward(inside, kind):
+    def forward(out, inside, kind):
         if direct == pair:
             return
-        spread_wait(inside.at[pl.ds(0, half - 1), shared_part], all_recv.at[kind])
+        spread_wait(out.at[pl.ds(0, half - 1), shared_part], all_recv.at[kind])
         mine = inside.at[pl.ds(side * half, half), shared_part]
         send(mine, mine, kind + 2, locate(lax.rem(here + half, devices)))
 
@@ -302,6 +318,8 @@
     for start in range(0, cells, TILE):
         part = slice(start, start + TILE)
         damage[:, part] = jnp.exp(-history[:, part])
+        for index, piece in enumerate(pieces_of(history[:, part])):
+            pieces[index, :, part] = piece
 
     fetch[6].wait()
     fetch[7].wait()
@@ -355,6 +373,17 @@
     leaves = jnp.where(steps_row > 0, home * padded + spots, -1)
     leaving = (iota((width, slots), 0) == leaves).astype(F32).astype(BF16)
 
+    def gather_out(split_of, out):
+        for start in range(0, cells, TILE):
+            part = slice(start, start + TILE)
+            rows = joined(leaving, split_of(part))
+            out[:, :, part] = rows.reshape(devices, padded, TILE)
+
+    gather_out(lambda part: [pieces[index, :, part] for index in range(3)], out_history)
+    in_history[pl.ds(here, 1)] = out_history[pl.ds(here, 1)]
+    send_shared(out_history, in_history, 1)
+    send_direct(out_history, in_history, 2, 1, devices)
+
     wanted_slot = iota((new_cap, LANES), 0)
     wanted = 2 * (here + devices * lax.shift_right_logical(wanted_slot, 1)) + (wanted_slot & 1)
     wanted_lane = iota((new_cap, LANES), 1)
@@ -367,23 +396,29 @@
     arrives = jnp.where(valid > 0.0, arrives, -1)
     coming = (iota((new_cap, width), 1) == arrives).astype(F32).astype(BF16)
 
-    def gather_out(values, out, inside):
-        for start in range(0, cells, TILE):
-            part = slice(start, start + TILE)
-            rows = picked(leaving, values[:, part])
-            out[:, :, part] = rows.reshape(devices, padded, TILE)
-        inside[pl.ds(here, 1)] = out[pl.ds(here, 1)]
-
-    gather_out(history, out_history, in_history)
-    send_shared(out_history, in_history, 1)
-    send_direct(out_history, in_history, 2, 1, devices)
+    results = (
+        (new_jump_ref, new_jump_hbm),
+        (new_load_ref, new_load_hbm),
+        (coming_ref, coming_hbm),
+        (kept_ref, kept_hbm),
+    )
+    leave = []
+    for index, (source, target) in enumerate(results):
+        leave.append(pltpu.make_async_copy(source, target, result_sems.at[index]))
+    coming_ref[...] = coming
+    leave[2].start()
 
     lax.fori_loop(EARLY, MAX_STEPS, advance, 0)
 
     others = devices - 1
     bounds = [1] + [1 + others * s // 31 for s in CHUNKS] + [devices]
 
-    gather_out(state, out_state, in_state)
+    gather_out(lambda part: pieces_of(state[:, part]), out_state)
+    rows_part = pl.ds(0, pair)
+    stays = pltpu.make_async_copy(
+        out_state.at[here, rows_part], in_state.at[here, rows_part], result_sems.at[4]
+    )
+    stays.start()
 
     def send_state(step):
         if step == 0:
@@ -498,16 +533,18 @@
         stage(phase, [(v, v) for v in iterate])
         halo_start(phase)
         if sweep == 0:
-            forward(in_history, 1)
+            forward(out_history, in_history, 1)
         send_state(sweep)
         if sweep == 1:
-            rows_wait(in_history, 1)
+            rows_wait(out_history, 1)
             for start in range(0, cells, TILE):
                 part = slice(start, start + TILE)
                 kept = picked(coming, in_history[:, :, part].reshape(width, TILE))
-                new_history_ref[:, part] = kept
+                kept_ref[:, part] = kept
+            leave[3].start()
         if sweep == 2:
-            forward(in_state, 4)
+            stays.wait()
+            forward(out_state, in_state, 4)
         halo_wait(phase)
         edges = edges_of(phase)
         iterate = solve_both([terms[c] + neighbours(phase, edges, iterate[c], c) for c in range(6)])
@@ -534,14 +571,13 @@
     increment = (radius_ref[0] * root - cross) / shifted
     for c in range(3):
         new_jump_ref[c] = jump[c] + correction[c] + increment * direction[c]
-    new_load_ref[...] = load_factor + increment
-
-    rows_wait(in_state, 4)
-    for start in range(0, cells, TILE):
-        part = slice(start, start + TILE)
-        moved = picked(coming, in_state[:, :, part].reshape(width, TILE))
-        new_state_ref[:, part] = moved
-
+    new_load_ref[...] = jnp.broadcast_to(load_factor + increment, new_load_ref.shape)
+    leave[0].start()
+    leave[1].start()
+
+    rows_wait(out_state, 4)
+    for copy in leave:
+        copy.wait()
     for phase in range(SWEEPS + 1):
         halo_wait_sends(phase)
     spread_wait(count_in.at[peers], all_send.at[0])
@@ -550,12 +586,81 @@
     spread_wait(sum_in.at[peers], all_send.at[7])
 
 
-def finish(jump_ref, load_ref, state_ref, history_ref, *outs):
-    new_jump_ref, new_load_ref, new_state_ref, new_history_ref = outs
-    new_jump_ref[...] = jump_ref[...]
-    new_load_ref[...] = load_ref[...]
-    new_state_ref[...] = state_ref[...]
-    new_history_ref[...] = jnp.maximum(history_ref[...], jnp.abs(state_ref[...]))
+def finish(
+    pair,
+    jump_hbm,
+    load_hbm,
+    coming_hbm,
+    kept_hbm,
+    rows_hbm,
+    new_jump_hbm,
+    new_load_ref,
+    new_state_hbm,
+    new_history_hbm,
+    jump_ref,
+    load_ref,
+    coming_ref,
+    kept_ref,
+    rows_ref,
+    state_ref,
+    in_sems,
+    row_sems,
+    out_sems,
+):
+    devices, padded, cells = rows_ref.shape
+    width = devices * padded
+    parts = [pl.ds(start, WIDE) for start in range(0, cells, WIDE)]
+    part_rows = pl.ds(0, pair)
+    whole = pl.ds(0, devices)
+    fetch = []
+    names = (
+        (coming_hbm, coming_ref),
+        (jump_hbm, jump_ref),
+        (load_hbm, load_ref),
+        (kept_hbm, kept_ref),
+    )
+    for index, (source, target) in enumerate(names):
+        fetch.append(pltpu.make_async_copy(source, target, in_sems.at[index]))
+    fetch[0].start()
+    rows = []
+    for index, part in enumerate(parts):
+        rows.append(
+            pltpu.make_async_copy(
+                rows_hbm.at[whole, part_rows, part],
+                rows_ref.at[whole, part_rows, part],
+                row_sems.at[index],
+            )
+        )
+        rows[-1].start()
+    for copy in fetch[1:]:
+        copy.start()
+    if pair < padded:
+        rows_ref[:, pair:, :] = jnp.zeros((devices, padded - pair, cells), F32)
+    stores = []
+
+    def store(source, target):
+        stores.append(pltpu.make_async_copy(source, target, out_sems.at[len(stores)]))
+        stores[-1].start()
+
+    fetch[0].wait()
+    coming = coming_ref[...]
+    for index, part in enumerate(parts):
+        rows[index].wait()
+        if index == 0:
+            fetch[1].wait()
+            store(jump_ref, new_jump_hbm)
+            fetch[2].wait()
+            new_load_ref[...] = load_ref[:, 0:1]
+            fetch[3].wait()
+        for start in range(index * WIDE, (index + 1) * WIDE, TILE):
+            tile = slice(start, start + TILE)
+            moved = picked(coming, rows_ref[:, :, tile].reshape(width, TILE))
+            state_ref[:, tile] = moved
+            kept_ref[:, tile] = jnp.maximum(kept_ref[:, tile], jnp.abs(moved))
+        store(state_ref.at[:, part], new_state_hbm.at[:, part])
+        store(kept_ref.at[:, part], new_history_hbm.at[:, part])
+    for copy in stores:
+        copy.wait()
 
 
 def on_device(
@@ -582,6 +687,16 @@
     phases = SWEEPS + 1
     shares = pair > 2 and nrow % 2 == 0 and slots <= (pair - 1) * devices
     direct = pair - 2 if shares else pair
+    width = devices * padded
+    landing = jax.ShapeDtypeStruct((devices, padded, cells), F32)
+    between = (
+        jax.ShapeDtypeStruct(jump.shape, F32),
+        jax.ShapeDtypeStruct((1, LANES), F32),
+        jax.ShapeDtypeStruct((new_cap, width), BF16),
+        jax.ShapeDtypeStruct((new_cap, cells), F32),
+        landing,
+    )
+    scratch = [pltpu.VMEM(shape.shape, shape.dtype) for shape in between]
     out_shape = (
         jax.ShapeDtypeStruct(jump.shape, F32),
         jax.ShapeDtypeStruct((1, 1), F32),
@@ -592,10 +707,12 @@
     hbm = pl.BlockSpec(memory_space=pltpu.HBM)
     results = pl.pallas_call(
         functools.partial(body, nrow, ncol, pair, direct),
-        out_shape=out_shape,
+        out_shape=between,
         in_specs=[hbm] * 12,
-        out_specs=(vmem,) * 4,
-        scratch_shapes=[
+        out_specs=(hbm,) * 5,
+        scratch_shapes=scratch[:4]
+        + [
+            pltpu.VMEM((3, slots, cells), BF16),
             pltpu.VMEM(jump.shape, F32),
             pltpu.VMEM(external.shape, F32),
             pltpu.VMEM(cohesive.shape, F32),
@@ -623,8 +740,8 @@
             pltpu.VMEM((devices, padded, cells), F32),
             pltpu.VMEM((devices, padded, cells), F32),
             pltpu.VMEM((devices, padded, cells), F32),
-            pltpu.VMEM((devices, padded, cells), F32),
             pltpu.SemaphoreType.DMA((12,)),
+            pltpu.SemaphoreType.DMA((5,)),
             pltpu.SemaphoreType.DMA((phases, 4)),
             pltpu.SemaphoreType.DMA((phases, 4)),
             pltpu.SemaphoreType.DMA((8,)),
@@ -648,10 +765,17 @@
         old_history,
     )
     new_jump, new_load, new_state, new_history = pl.pallas_call(
-        finish,
+        functools.partial(finish, pair),
         out_shape=out_shape,
-        in_specs=[vmem] * 4,
-        out_specs=(vmem,) * 4,
+        in_specs=[hbm] * 5,
+        out_specs=(hbm, vmem, hbm, hbm),
+        scratch_shapes=scratch
+        + [
+            pltpu.VMEM((new_cap, cells), F32),
+            pltpu.SemaphoreType.DMA((4,)),
+            pltpu.SemaphoreType.DMA((cells // WIDE,)),
+            pltpu.SemaphoreType.DMA((2 * (cells // WIDE) + 1,)),
+        ],
         compiler_params=pltpu.CompilerParams(vmem_limit_bytes=GRANT),
     )(*results)
     return new_jump, new_load.reshape(1), new_state, new_history

time: 63.5 us -> 62.6 us (0.986)
  Pallas kernels: 61.4 us -> 60.5 us
    pallas_call x1, Pallas kernels: 58.6 us -> 56.9 us  [on_device(): pl.pallas_call(functools.partial(body, nrow, ncol, pair, direct), out_sha...]
    pallas_call x1, Pallas kernels: 2.8 us -> 3.6 us  [on_device(): pl.pallas_call(functools.partial(finish, pair), out_shape=out_shape, in_s...]
where the time goes in v3:
time: 62.6 us; the launch traced here: 62.4 us
  Pallas kernels  60.5 us (97%)
  between operations  1.93 us (3%)
    pallas_call x1, Pallas kernels, on_device(): pl.pallas_call(functools.partial(body, nrow, ncol, pair, direct), out_sha...  56.9 us
    pallas_call x1, Pallas kernels, on_device(): pl.pallas_call(functools.partial(finish, pair), out_shape=out_shape, in_s...  3.6 us

profile of v3, /device:TPU:0, one launch (start us, length us, event | category | flops | bytes accessed | tf_op | source)
XLA Modules:
  0.0 62.4 jit_solution(1984109645528607205)
XLA Ops:
  1.9 56.9 %shard_map.147 = (f32[3,64,128]{2,1,0:T(8,128)}, f32[1,128]{1,0:T(1,128)}, bf16[80,256]{1,0:T(8,128)(2,1)}, f32[80,1536]{1,0:T(8,128)}, f32[32,8,1536]{2,1,0:T(8,128)}) custom-call(f32[3,64,128]{2,1,0:T(8,128)} %jump_hbm.1, f32[3,64,128]{2,1,0:T(8,128)} %external_hbm.1, f32[64,128]{1,0:T(8,128)} %cohesive_hbm.1, s32[2,64,128]{2,1,0:T(8,128)} %bond_hbm.1, ...), custom_call_target="tpu_custom_call" | custom-call | tf_op jit(solution)/shard_map/pallas_call | solution.py:708
  58.8 3.6 %shard_map.148 = (f32[3,64,128]{2,1,0:T(8,128)}, f32[1,1]{1,0:T(1,128)}, f32[80,1536]{1,0:T(8,128)}, f32[80,1536]{1,0:T(8,128)}) custom-call(f32[3,64,128]{2,1,0:T(8,128)} %get-tuple-element.13.jump_hbm, f32[1,128]{1,0:T(1,128)} %get-tuple-element.14.load_hbm, bf16[80,256]{1,0:T(8,128)(2,1)} %get-tuple-element.15.coming_hbm, ...), custom_call_target="tpu_custom_call" | custom-call | tf_op jit(solution)/shard_map/pallas_call | solution.py:767

commit v4 on v3

--- a/solution.py
+++ b/solution.py
@@ -532,9 +532,9 @@
         phase = sweep + 1
         stage(phase, [(v, v) for v in iterate])
         halo_start(phase)
+        send_state(sweep)
         if sweep == 0:
             forward(out_history, in_history, 1)
-        send_state(sweep)
         if sweep == 1:
             rows_wait(out_history, 1)
             for start in range(0, cells, TILE):

time: 62.6 us -> 62.6 us (level)
  no operation moved by 1% of the time
where the time goes in v4:
time: 62.6 us; the launch traced here: 62.4 us
  Pallas kernels  60.5 us (97%)
  between operations  1.93 us (3%)
    pallas_call x1, Pallas kernels, on_device(): pl.pallas_call(functools.partial(body, nrow, ncol, pair, direct), out_sha...  56.9 us
    pallas_call x1, Pallas kernels, on_device(): pl.pallas_call(functools.partial(finish, pair), out_shape=out_shape, in_s...  3.6 us

profile of v4, /device:TPU:0, one launch (start us, length us, event | category | flops | bytes accessed | tf_op | source)
XLA Modules:
  0.0 62.4 jit_solution(18425434011984990668)
XLA Ops:
  1.9 56.9 %shard_map.147 = (f32[3,64,128]{2,1,0:T(8,128)}, f32[1,128]{1,0:T(1,128)}, bf16[80,256]{1,0:T(8,128)(2,1)}, f32[80,1536]{1,0:T(8,128)}, f32[32,8,1536]{2,1,0:T(8,128)}) custom-call(f32[3,64,128]{2,1,0:T(8,128)} %jump_hbm.1, f32[3,64,128]{2,1,0:T(8,128)} %external_hbm.1, f32[64,128]{1,0:T(8,128)} %cohesive_hbm.1, s32[2,64,128]{2,1,0:T(8,128)} %bond_hbm.1, ...), custom_call_target="tpu_custom_call" | custom-call | tf_op jit(solution)/shard_map/pallas_call | solution.py:708
  58.8 3.6 %shard_map.148 = (f32[3,64,128]{2,1,0:T(8,128)}, f32[1,1]{1,0:T(1,128)}, f32[80,1536]{1,0:T(8,128)}, f32[80,1536]{1,0:T(8,128)}) custom-call(f32[3,64,128]{2,1,0:T(8,128)} %get-tuple-element.13.jump_hbm, f32[1,128]{1,0:T(1,128)} %get-tuple-element.14.load_hbm, bf16[80,256]{1,0:T(8,128)(2,1)} %get-tuple-element.15.coming_hbm, ...), custom_call_target="tpu_custom_call" | custom-call | tf_op jit(solution)/shard_map/pallas_call | solution.py:767
